TPU v7x, 32 devices: a whole 2x2x4 slice. The times are simulated.
32 devices in a mesh: tissue: 2 (over core), row: 4 (over y, x), col: 4 (over z).
Axes of the slice: x: 2, y: 2, z: 4, core: 2. Of those that a mesh axis runs over, the one named last changes fastest.
Arguments:
- expr: float32 [1200, 16384], P(('tissue', 'row'), 'col'), parts along dimension 0, may hold values from -48 to 88
- win_genes: int32 [256], replicated, may hold values from 0 to 16383, as said below
Outputs:
- margin: float32 [512, 16384], P(('tissue', 'row'), 'col'), parts along dimension 0
- degree: float32 [32768], P(('tissue', 'col')), parts along dimension 0
There are 2 independent parts, one for each index of `tissue`. A program takes and returns all parts, laid end to end along the dimension named above; an argument that names none is the same for every part. Nothing has to cross between parts.
Inputs may be any that keep to these rules, and one draw needn't show every extreme that they name: `win_genes`: 256 distinct gene numbers.
All inputs are finite; a program needn't handle non-finite values.
Results may differ from a plain program's by a relative error of at most 0.00077.
Values may be sent and summed in bfloat16 or wider, within the bound.
A program may use at most 128 MiB of HBM per device.

v0:
```python
import jax
import jax.numpy as jnp
from jax import lax
from jax.sharding import PartitionSpec as P


def power_eight(corr):
    half = (1.0 + corr) * 0.5
    half = half * half
    half = half * half
    return half * half


def inner_first(left, right):
    return lax.dot_general(
        left, right, (((0,), (0,)), ((), ())), preferred_element_type=jnp.float32
    )


def body(expr, win_genes):
    n_row = lax.axis_size("row")
    samples_all = expr.shape[0] * n_row
    totals = lax.psum(jnp.sum(expr, axis=0), "row")
    centered = expr - totals / samples_all
    squares = lax.psum(jnp.sum(centered * centered, axis=0), "row")
    z = (centered / jnp.sqrt(squares + 1e-06)).astype(jnp.bfloat16)
    zcol = lax.all_gather(z, "row", axis=0, tiled=True)
    width = zcol.shape[1]
    slab = width // n_row
    row_id = lax.axis_index("row")
    col_id = lax.axis_index("col")
    zpiece = lax.dynamic_slice_in_dim(zcol, row_id * slab, slab, 1)
    zrows = lax.all_gather(zpiece, "col", axis=1, tiled=True)
    adj = power_eight(inner_first(zrows, zcol)).astype(jnp.bfloat16)
    local_rows = jnp.arange(zrows.shape[1], dtype=jnp.int32)
    genes_i = local_rows // slab * width + row_id * slab + local_rows % slab
    genes_j = col_id * width + jnp.arange(width, dtype=jnp.int32)
    keep = genes_i[:, None] != genes_j[None, :]
    partial_degree = jnp.sum(jnp.where(keep, adj.astype(jnp.float32), jnp.float32(0.0)), axis=0)
    degree = lax.psum(partial_degree, "row")
    offsets = win_genes - col_id * width
    inside = (offsets >= 0) & (offsets < width)
    clipped = jnp.clip(offsets, 0, width - 1)
    picked = jnp.take(zcol, clipped, axis=1)
    terms = jnp.where(inside[None, :], picked, jnp.zeros((), jnp.bfloat16))
    zwin = lax.psum(terms, "col").astype(jnp.float32).astype(jnp.bfloat16)
    panel = power_eight(inner_first(zrows, zwin)).astype(jnp.bfloat16)
    margin = lax.psum_scatter(inner_first(panel, adj), "row", scatter_dimension=0, tiled=True)
    return (margin, degree)


def solution(mesh):
    in_specs = (P(("tissue", "row"), "col"), P())
    out_specs = (P(("tissue", "row"), "col"), P(("tissue", "col")))
    return jax.shard_map(body, mesh=mesh, in_specs=in_specs, out_specs=out_specs, check_vma=False)
```

profile of v0, /device:TPU:2, one launch (start us, length us, event | category | flops | bytes accessed | tf_op | source)
XLA Modules:
  0.0 333.6 jit_solution(13726724207227180818)
XLA Ops:
  7.2 0.0 copy-start
  7.2 0.0 all-gather.6.cloned.1.call-start
  7.2 2.0 reduce_sum.27
  9.2 14.1 %psum.28 = f32[4096]{0:T(1024)S(1)} all-reduce(f32[4096]{0:T(1024)S(1)} %reduce_sum.27), channel_id=1, replica_groups=mesh['tissue'=2,'row'=4,'col'=4] {'row'}, use_global_device_ids=true, to_apply=%region_1.0 | all-reduce | flops 4096 | bytes 32768 | tf_op jit(solution)/shard_map/psum | solution.py:23
  23.3 2.0 multiply_reduce_fusion
  25.3 15.1 %psum.29 = f32[4096]{0:T(1024)S(1)} all-reduce(f32[4096]{0:T(1024)S(1)} %multiply_reduce_fusion), channel_id=1, replica_groups=mesh['tissue'=2,'row'=4,'col'=4] {'row'}, use_global_device_ids=true, to_apply=%region_3.0 | all-reduce | flops 4096 | bytes 32768 | tf_op jit(solution)/shard_map/psum | solution.py:25
  40.4 0.0 copy-done
  40.5 1.3 fusion.5
  41.8 0.0 all-gather.6.cloned.1.call-update
  41.8 0.0 all-gather.4.cloned.1.call-start
  41.9 0.0 copy-start.1
  41.9 60.3 %all-gather.6.cloned.1.call-done = bf16[4,150,4096]{2,1,0:T(8,128)(2,1)} async-done(((bf16[1,150,4096]{2,1,0:T(8,128)(2,1)}), bf16[4,150,4096]{2,1,0:T(8,128)(2,1)}) %all-gather.6.cloned.1.call-update) | async-done | bytes 4915216 | tf_op jit(solution)/shard_map/all_gather | solution.py:27
  102.2 6.0 %reshape.49 = bf16[600,4096]{1,0:T(8,128)(2,1)} reshape(bf16[4,150,4096]{2,1,0:T(8,128)(2,1)} %all-gather.6.cloned.1.call-done) | data formatting | bytes 9830400
  108.2 2.4 constant_dynamic-slice_fusion
  110.6 0.0 all-gather.4.cloned.1.call-update
  110.7 0.0 all-reduce.2.cloned.1.call-start
  110.7 0.0 copy-done.1
  110.8 7.8 %copy.6 = bf16[600,4096]{0,1:T(8,128)(2,1)} copy(bf16[600,4096]{1,0:T(8,128)(2,1)} %reshape.49) | data formatting | bytes 9830400
  118.5 4.9 %gather_fusion = bf16[256,600]{1,0:T(8,128)(2,1)S(1)} fusion(bf16[600,4096]{0,1:T(8,128)(2,1)} %copy.6, s32[1024]{0:T(1024)S(1)} %pad_clamp_fusion), kind=kCustom, calls=%fused_computation | custom fusion | bytes 615424 | tf_op jit(solution)/shard_map/jit(_take)/gather | solution.py:44
  123.4 0.9 select_bitcast_fusion
  124.3 0.0 all-reduce.2.cloned.1.call-update
  124.3 0.2 reduce-scatter.2.cloned.1.call-start
  124.6 78.9 %all-gather.4.cloned.1.call-done = bf16[600,4096]{1,0:T(8,128)(2,1)} async-done(((bf16[600,1024]{1,0:T(8,128)(2,1)}), bf16[600,4096]{1,0:T(8,128)(2,1)}) %all-gather.4.cloned.1.call-update) | async-done | bytes 4915216 | tf_op jit(solution)/shard_map/all_gather | solution.py:33
  203.4 45.1 %select_reduce_fusion = (f32[4096]{0:T(1024)S(1)}, bf16[4096,4096]{1,0:T(8,128)(2,1)}) fusion(s32[4096]{0:T(1024)S(1)} %get-tuple-element.8, s32[4096]{0:T(1024)S(1)} %get-tuple-element.7, bf16[600,4096]{1,0:T(8,128)(2,1)} %all-gather.4.cloned.1.call-done, bf16[600,4096]{1,0:T(8,128)(2,1)} %reshape.49), kind=kOutput, calls=%fused_computation.1 | convolution fusion | flops 20300427264 | bytes 43433984 | tf_op jit(solution)/shard_map/dot_general | solution.py:15
  248.6 0.0 all-reduce.2.cloned.1.call-done
  248.6 27.1 %fusion.6 = f32[256,4096]{1,0:T(8,128)} fusion(bf16[4096,4096]{1,0:T(8,128)(2,1)} %get-tuple-element.6, bf16[600,4096]{1,0:T(8,128)(2,1)} %all-gather.4.cloned.1.call-done, bf16[600,256]{0,1:T(8,128)(2,1)} %all-reduce.2.cloned.1.call-done), kind=kOutput, calls=%fused_computation.12 | convolution fusion | flops 9854517248 | bytes 42971136 | tf_op jit(solution)/shard_map/dot_general | solution.py:15
  275.7 0.0 reduce-scatter.2.cloned.1.call-update
  275.7 15.3 %psum.31 = f32[4096]{0:T(1024)} all-reduce(f32[4096]{0:T(1024)S(1)} %get-tuple-element.5), channel_id=1, replica_groups=mesh['tissue'=2,'row'=4,'col'=4] {'row'}, use_global_device_ids=true, to_apply=%region_7.8 | all-reduce | flops 4096 | bytes 32768 | tf_op jit(solution)/shard_map/psum | solution.py:40
  291.0 36.0 %reduce-scatter.2.cloned.1.call-done = f32[64,4096]{1,0:T(8,128)} async-done(((f32[256,4096]{1,0:T(8,128)}), f32[64,4096]{1,0:T(8,128)}) %reduce-scatter.2.cloned.1.call-update) | async-done | bytes 1048592 | tf_op jit(solution)/shard_map/reduce_scatter | solution.py:48
  (5 shorter events, 0.0 us)
Async XLA Ops:
  7.2 33.3 %copy-start = (f32[150,4096]{1,0:T(8,128)S(1)}, f32[150,4096]{1,0:T(8,128)}, u32[]{:S(2)}) copy-start(f32[150,4096]{1,0:T(8,128)} %param.2) | copy-start | bytes 7372804
  7.2 95.0 %all-gather.6.cloned.1.call-start = ((), (), s32[]{:S(2)}) async-start(), calls=%async_computation.4 | async-start | bytes 6225920 | tf_op jit(solution)/shard_map/all_gather | solution.py:27
  41.8 161.6 %all-gather.4.cloned.1.call-start = ((), (), s32[]{:S(2)}) async-start(), calls=%async_computation.1 | async-start | bytes 6144000 | tf_op jit(solution)/shard_map/all_gather | solution.py:33
  41.9 68.8 %copy-start.1 = (s32[256]{0:T(256)S(1)}, s32[256]{0:T(256)}, u32[]{:S(2)}) copy-start(s32[256]{0:T(256)} %param.3) | copy-start | bytes 3076
  110.7 137.9 %all-reduce.2.cloned.1.call-start = ((), (), s32[]{:S(2)}) async-start(), calls=%async_computation.2 | async-start | bytes 655360 | tf_op jit(solution)/shard_map/psum | solution.py:46
  124.3 202.7 %reduce-scatter.2.cloned.1.call-start = ((), (), s32[]{:S(2)}) async-start(), calls=%async_computation.3 | async-start | bytes 5242880 | tf_op jit(solution)/shard_map/reduce_scatter | solution.py:48
Sparse Core Ops, SparseCore 0:
  41.9 60.2 all-gather.5
  110.8 92.6 all-gather.3
  206.4 34.8 all-reduce.1
  275.8 51.1 reduce-scatter.1
where the time goes:
time: 336 us; the launch traced here: 334 us
  waiting for transfers between devices  175 us (52%)
  matrix products  72.2 us (21%)
  blocking collectives  44.5 us (13%)
  local copies, waits for them, and re-layouts  21.1 us (6%)
  between operations  13.8 us (4%)
  other arithmetic  6.23 us (2%)
    all_gather x1, waiting for transfers between devices, body(): zrows = lax.all_gather(zpiece, 'col', axis=1, tiled=True)  78.9 us
    dot_general x2, matrix products, inner_first(): lax.dot_general(left, right, (((0,), (0,)), ((), ())), preferred_element_...  72.2 us
    all_gather x1, waiting for transfers between devices, body(): zcol = lax.all_gather(z, 'row', axis=0, tiled=True)  60.3 us
    reduce_scatter x1, waiting for transfers between devices, body(): lax.psum_scatter(inner_first(panel, adj), 'row', scatter_dimension=0, til...  36 us
    psum x1, blocking collectives, body(): degree = lax.psum(partial_degree, 'row')  15.3 us
    psum x1, blocking collectives, body(): squares = lax.psum(jnp.sum(centered * centered, axis=0), 'row')  15.1 us
    psum x1, blocking collectives, body(): totals = lax.psum(jnp.sum(expr, axis=0), 'row')  14.1 us
    unnamed x6, local copies, waits for them, and re-layouts  13.8 us
  transfers between devices with their start and end apart: 4, of which 3 were waited for; matrix products, arithmetic and copies ran while one was open for 18% of the time, Pallas kernels for 0%

commit v1 on v0

v1 whole, which is shorter than its diff:
```python
import functools

import jax
import jax.numpy as jnp
from jax import lax
from jax.experimental import pallas as pl
from jax.experimental.pallas import tpu as pltpu
from jax.sharding import PartitionSpec as P

MESH = pl.DeviceIdType.MESH
F32 = jnp.float32
BF16 = jnp.bfloat16


def power_eight(corr):
    half = (1.0 + corr) * 0.5
    half = half * half
    half = half * half
    return half * half


def flip(r, d):
    out = r
    for b in range(6):
        bit = 1 << b
        out = out + ((d // bit) % 2) * (1 - 2 * ((r // bit) % 2)) * bit
    return out


def dot(a, b, dims=((1,), (0,))):
    return lax.dot_general(a, b, (dims, ((), ())), preferred_element_type=F32)


def kernel(R, C, eps, expr, win, out, dego,
           stats, zl, zcol, zrt, zw, zwr, zwt, zt, pbuf, macc, rs, degb, degr,
           s_st, r_st, s_aa, r_aa, s_ga, r_ga, s_zc, r_zc, s_zr, r_zr,
           s_up, r_up, s_dn, r_dn, s_rs, r_rs, s_dg, r_dg):
    r = lax.axis_index("row")
    c = lax.axis_index("col")
    S, width = expr.shape
    pad = zl.shape[0]
    slab = width // R
    W = zw.shape[2]
    per = W // R
    NC, chunk = zrt.shape[1], zrt.shape[2]

    barrier = pltpu.get_barrier_semaphore()
    for d in range(1, R):
        pl.semaphore_signal(barrier, inc=1, device_id={"row": flip(r, d)}, device_id_type=MESH)
    for d in range(1, C):
        pl.semaphore_signal(barrier, inc=1, device_id={"col": lax.rem(c + d, C)}, device_id_type=MESH)

    for j in range(R):
        cols = slice(j * slab, (j + 1) * slab)
        x = expr[:, cols]
        total = jnp.sum(x, axis=0, keepdims=True)
        dev = x - total * (1.0 / S)
        stats[0, 0:1, cols] = total
        stats[0, 1:2, cols] = jnp.sum(dev * dev, axis=0, keepdims=True)
    pl.semaphore_wait(barrier, R + C - 2)

    def rowcopy(src, dst, ss, rr, d):
        return pltpu.make_async_remote_copy(
            src_ref=src, dst_ref=dst, send_sem=ss, recv_sem=rr,
            device_id={"row": flip(r, d)}, device_id_type=MESH)

    def colcopy(src, dst, ss, rr, peer):
        return pltpu.make_async_remote_copy(
            src_ref=src, dst_ref=dst, send_sem=ss, recv_sem=rr,
            device_id={"col": peer}, device_id_type=MESH)

    st = [rowcopy(stats.at[0], stats.at[d], s_st.at[d], r_st.at[d], d) for d in range(1, R)]
    for cp in st:
        cp.start()
    macc[...] = jnp.zeros_like(macc)
    zl[pad - 16:pad, :] = jnp.zeros((16, width), BF16)
    pbuf[...] = jnp.ones_like(pbuf)
    for cp in st:
        cp.wait_recv()

    for j in range(R):
        cols = slice(j * slab, (j + 1) * slab)
        total = stats[0, 0:1, cols]
        for d in range(1, R):
            total = total + stats[d, 0:1, cols]
        mean = total / (S * R)
        sq = jnp.zeros_like(mean)
        for d in range(R):
            gap = stats[d, 0:1, cols] * (1.0 / S) - mean
            sq = sq + (stats[d, 1:2, cols] + S * gap * gap)
        inv = 1.0 / jnp.sqrt(sq + eps)
        zl[0:S, cols] = ((expr[:, cols] - mean) * inv).astype(BF16)

    mine = pl.ds(pl.multiple_of(r * pad, 16), pad)
    aa = []
    for d in range(1, R):
        q = flip(r, d)
        aa.append(rowcopy(zl.at[:, pl.ds(pl.multiple_of(q * slab, 128), slab)],
                          zcol.at[q, mine, :], s_aa.at[d], r_aa.at[d], d))
        aa[-1].start()
    zcol[r, mine, :] = zl[:, pl.ds(pl.multiple_of(r * slab, 128), slab)]

    pick = jnp.zeros((pad, W), F32)
    for j in range(R):
        gene = lax.broadcasted_iota(jnp.int32, (slab, W), 0) + (c * width + j * slab)
        onehot = jnp.where(gene == win[...], 1.0, 0.0).astype(BF16)
        pick = pick + dot(zl[:, j * slab:(j + 1) * slab], onehot)
    zw[0] = pick.astype(BF16)
    zc = []
    for d in range(1, C):
        zc.append(colcopy(zw.at[0], zw.at[d], s_zc.at[d], r_zc.at[d], lax.rem(c + d, C)))
        zc[-1].start()

    for cp in aa:
        cp.wait_recv()
    zr_own = zcol.at[r]
    lo, hi = c > 0, c < C - 1

    def up(s, k):
        i = c - s
        return colcopy(zrt.at[i, k], zrt.at[i, k], s_up.at[s, k], r_up.at[s, k], c + 1)

    def up_in(s, k):
        i = c - s
        return colcopy(zrt.at[i, k], zrt.at[i, k], s_up.at[s - 1, k], r_up.at[s - 1, k], c + 1)

    def down(s, k):
        i = c + s
        return colcopy(zrt.at[i, k], zrt.at[i, k], s_dn.at[s, k], r_dn.at[s, k], c - 1)

    def down_in(s, k):
        i = c + s
        return colcopy(zrt.at[i, k], zrt.at[i, k], s_dn.at[s - 1, k], r_dn.at[s - 1, k], c - 1)

    for k in range(NC):
        zrt[c, k] = zr_own[:, k * chunk:(k + 1) * chunk].T

        @pl.when(hi)
        def _():
            up(0, k).start()

        @pl.when(lo)
        def _():
            down(0, k).start()

    ga = []
    for d in range(1, R):
        ga.append(rowcopy(zcol.at[r], zcol.at[r], s_ga.at[d], r_ga.at[d], d))

    tot = zw[0].astype(F32)
    for cp in zc:
        cp.wait_recv()
    for d in range(1, C):
        tot = tot + zw[d].astype(F32)
    zwr[0] = tot.astype(BF16)
    zr = []
    for d in range(1, R):
        zr.append(rowcopy(zwr.at[0], zwr.at[d], s_zr.at[d], r_zr.at[d], d))
        zr[-1].start()
    for cp in ga:
        cp.start()
    for cp in zr:
        cp.wait_recv()
    for d in range(R):
        zwt[pl.ds(pl.multiple_of(flip(r, d) * pad, 16), pad), :] = zwr[d]
    zt[...] = zwt[...].T

    def compute(i, k, d_lo, d_hi):
        pbuf[0:W, :] = power_eight(dot(zt[...], zrt[i, k], ((1,), (1,)))).astype(BF16)

        def one(d, _):
            j = flip(r, d)
            adj = power_eight(dot(zrt[i, k], zcol[j])).astype(BF16)
            macc[j] += dot(pbuf[...], adj)
            return 0
        lax.fori_loop(d_lo, d_hi, one, 0)

    def arrive(s, k):
        @pl.when(c - s >= 0)
        def _():
            up_in(s, k).wait_recv()

            @pl.when(hi)
            def _():
                up(s, k).start()

        @pl.when(c + s < C)
        def _():
            down_in(s, k).wait_recv()

            @pl.when(lo)
            def _():
                down(s, k).start()

    def phase(s, t_lo, t_hi, start, d_hi):
        def step(k, _):
            arrive(s, k)

            def each(t, _):
                i = c + (1 - 2 * (t % 2)) * ((t + 1) // 2)

                @pl.when((i >= 0) & (i < C))
                def _():
                    compute(i, k, start(t), d_hi)
                return 0
            lax.fori_loop(t_lo, t_hi, each, 0)
            return 0
        lax.fori_loop(0, NC, step, 0)

    def own(k, _):
        compute(c, k, 0, 1)
        return 0
    lax.fori_loop(0, NC, own, 0)

    def pass_on(k, _):
        arrive(1, k)
        return 0
    lax.fori_loop(0, NC, pass_on, 0)
    for cp in ga[:-1]:
        cp.wait_recv()
    phase(2, 0, 3, lambda t: jnp.where(t == 0, 1, 0), R - 1)
    ga[-1].wait_recv()
    phase(3, 0, 7, lambda t: jnp.where(t < 3, R - 1, 0), R)
    if C > 4:
        def later(s, _):
            phase(s, 2 * s - 1, 2 * s + 1, lambda t: 0, R)
            return 0
        lax.fori_loop(4, C, later, 0)

    out_cp = []
    for d in range(1, R):
        q = pl.multiple_of(flip(r, d) * per, 8)
        for j in range(R):
            out_cp.append(rowcopy(macc.at[j, pl.ds(q, per), :], rs.at[d, j],
                                  s_rs.at[d, j], r_rs.at[d, j], d))
            out_cp[-1].start()
    for j in range(R):
        degb[j] = macc[j, W:W + 1, :]
    zs = zcol[r].astype(F32)
    self_term = power_eight(jnp.sum(zs * zs, axis=0, keepdims=True))
    degb[r] = degb[r] - self_term.astype(BF16).astype(F32)
    dg = []
    for d in range(1, R):
        dg.append(rowcopy(degb, degr.at[d], s_dg.at[d], r_dg.at[d], d))
        dg[-1].start()
    own_rows = pl.ds(pl.multiple_of(r * per, 8), per)
    for j in range(R):
        total = macc[j, own_rows, :]
        for d in range(1, R):
            out_cp[(d - 1) * R + j].wait_recv()
            total = total + rs[d, j]
        out[:, j * slab:(j + 1) * slab] = total
    for cp in dg:
        cp.wait_recv()
    for j in range(R):
        total = degb[j]
        for d in range(1, R):
            total = total + degr[d, j]
        dego[:, j * slab:(j + 1) * slab] = total

    for cp in st + aa + zc + zr + ga + out_cp + dg:
        cp.wait_send()

    def drain(s, _):
        def each(k, _):
            @pl.when(hi & (c - s >= 0))
            def _():
                up(s, k).wait_send()

            @pl.when(lo & (c + s < C))
            def _():
                down(s, k).wait_send()
            return 0
        lax.fori_loop(0, NC, each, 0)
        return 0
    lax.fori_loop(0, C - 1, drain, 0)


def solution(mesh):
    R, C = mesh.shape["row"], mesh.shape["col"]

    def body(expr, win):
        S, width = expr.shape
        W = win.shape[0]
        pad = (S + 15) // 16 * 16
        slab = width // R
        chunk = min(256, slab)
        NC = slab // chunk
        V = pltpu.VMEM
        dma = pltpu.SemaphoreType.DMA
        vm = pl.BlockSpec(memory_space=pltpu.VMEM)
        margin, degree = pl.pallas_call(
            functools.partial(kernel, R, C, 1e-6),
            out_shape=(jax.ShapeDtypeStruct((W // R, width), F32),
                       jax.ShapeDtypeStruct((1, width), F32)),
            in_specs=[vm, vm],
            out_specs=(vm, vm),
            scratch_shapes=[
                V((R, 2, width), F32),
                V((pad, width), BF16),
                V((R, R * pad, slab), BF16),
                V((C, NC, chunk, R * pad), BF16),
                V((C, pad, W), BF16),
                V((R, pad, W), BF16),
                V((R * pad, W), BF16),
                V((W, R * pad), BF16),
                V((W + 16, chunk), BF16),
                V((R, W + 16, slab), F32),
                V((R, R, W // R, slab), F32),
                V((R, 1, slab), F32),
                V((R, R, 1, slab), F32),
                dma((R,)), dma((R,)), dma((R,)), dma((R,)), dma((R,)), dma((R,)),
                dma((C,)), dma((C,)), dma((R,)), dma((R,)),
                dma((C, NC)), dma((C, NC)), dma((C, NC)), dma((C, NC)),
                dma((R, R)), dma((R, R)), dma((R,)), dma((R,)),
            ],
            compiler_params=pltpu.CompilerParams(
                collective_id=0, has_side_effects=True, vmem_limit_bytes=56 << 20),
        )(expr, win.reshape(1, W))
        return margin, degree.reshape(width)

    in_specs = (P(("tissue", "row"), "col"), P())
    out_specs = (P(("tissue", "row"), "col"), P(("tissue", "col")))
    return jax.shard_map(body, mesh=mesh, in_specs=in_specs, out_specs=out_specs, check_vma=False)
```

time: 336 us -> 188 us (0.56)
  Pallas kernels: 0 us -> 183 us
  waiting for transfers between devices: 175 us -> 0 us
  matrix products: 72.2 us -> 0 us
  blocking collectives: 44.5 us -> 0 us
  local copies, waits for them, and re-layouts: 21.1 us -> 3.59 us
  between operations: 13.8 us -> 0.64 us
  other arithmetic: 6.23 us -> 0 us
    pallas_call x0 -> x1, Pallas kernels: none -> 183 us  [body(): pl.pallas_call(functools.partial(kernel, R, C, 1e-06), out_shape=(jax.Sha...]
    all_gather x2 -> x0, waiting for transfers between devices: 139 us -> none  [the longest x1 78.9 us: body(): zrows = lax.all_gather(zpiece, 'col', axis=1, tiled=True)]
    dot_general x2 -> x0, matrix products: 72.2 us -> none  [inner_first(): lax.dot_general(left, right, (((0,), (0,)), ((), ())), preferred_element_...]
    psum x3 -> x0, blocking collectives: 44.5 us -> none  [the longest x1 15.3 us: body(): degree = lax.psum(partial_degree, 'row')]
    reduce_scatter x1 -> x0, waiting for transfers between devices: 36 us -> none  [body(): lax.psum_scatter(inner_first(panel, adj), 'row', scatter_dimension=0, til...]
    unnamed x6 -> x2, local copies, waits for them, and re-layouts: 13.8 us -> 3.59 us
    gather x1 -> x0, local copies, waits for them, and re-layouts: 4.89 us -> none  [body(): picked = jnp.take(zcol, clipped, axis=1)]
    reduce_sum x2 -> x0, other arithmetic: 3.97 us -> none  [the longest x1 1.99 us: body(): totals = lax.psum(jnp.sum(expr, axis=0), 'row')]
  transfers between devices with their start and end apart: 4 -> 0, of which waited for: 3 -> 0; matrix products, arithmetic and copies ran while one was open for 18% -> 0% of each run, Pallas kernels for 0% -> 0%
where the time goes in v1:
time: 188 us
  Pallas kernels  183 us (97%)
  local copies, waits for them, and re-layouts  3.59 us (2%)
    pallas_call x1, Pallas kernels, body(): pl.pallas_call(functools.partial(kernel, R, C, 1e-06), out_shape=(jax.Sha...  183 us

profile of v1, /device:TPU:2, one launch (start us, length us, event | category | flops | bytes accessed | tf_op | source)
XLA Modules:
  0.0 187.6 jit_solution(475050305389309627)
XLA Ops:
  0.6 183.4 %shard_map.41 = (f32[64,4096]{1,0:T(8,128)}, f32[1,4096]{1,0:T(1,128)}) custom-call(f32[150,4096]{1,0:T(8,128)} %expr.1, s32[1,256]{1,0:T(1,128)} %bitcast.3), custom_call_target="tpu_custom_call" | custom-call | tf_op jit(solution)/shard_map/pallas_call | solution.py:292
  184.1 2.3 %copy.6 = f32[64,4096]{1,0:T(8,128)} copy(f32[64,4096]{1,0:T(8,128)} %get-tuple-element.8) | data formatting | bytes 2097152
  186.3 1.3 copy.7

commit v2 on v1

--- a/solution.py
+++ b/solution.py
@@ -32,7 +32,7 @@
 
 
 def kernel(R, C, eps, expr, win, out, dego,
-           stats, zl, zcol, zrt, zw, zwr, zwt, zt, pbuf, macc, rs, degb, degr,
+           stats, zl, zcol, zrt, zw, zwr, zwt, pbuf, macc, rs, degb, degr,
            s_st, r_st, s_aa, r_aa, s_ga, r_ga, s_zc, r_zc, s_zr, r_zr,
            s_up, r_up, s_dn, r_dn, s_rs, r_rs, s_dg, r_dg):
     r = lax.axis_index("row")
@@ -93,11 +93,14 @@
 
     mine = pl.ds(pl.multiple_of(r * pad, 16), pad)
     aa = []
-    for d in range(1, R):
-        q = flip(r, d)
-        aa.append(rowcopy(zl.at[:, pl.ds(pl.multiple_of(q * slab, 128), slab)],
-                          zcol.at[q, mine, :], s_aa.at[d], r_aa.at[d], d))
-        aa[-1].start()
+    for k in range(NC):
+        for d in range(1, R):
+            q = flip(r, d)
+            at = pl.multiple_of(q * slab + k * chunk, 128)
+            aa.append(rowcopy(zl.at[:, pl.ds(at, chunk)],
+                              zcol.at[q, mine, k * chunk:(k + 1) * chunk],
+                              s_aa.at[k, d], r_aa.at[k, d], d))
+            aa[-1].start()
     zcol[r, mine, :] = zl[:, pl.ds(pl.multiple_of(r * slab, 128), slab)]
 
     pick = jnp.zeros((pad, W), F32)
@@ -111,8 +114,6 @@
         zc.append(colcopy(zw.at[0], zw.at[d], s_zc.at[d], r_zc.at[d], lax.rem(c + d, C)))
         zc[-1].start()
 
-    for cp in aa:
-        cp.wait_recv()
     zr_own = zcol.at[r]
     lo, hi = c > 0, c < C - 1
 
@@ -133,6 +134,8 @@
         return colcopy(zrt.at[i, k], zrt.at[i, k], s_dn.at[s - 1, k], r_dn.at[s - 1, k], c - 1)
 
     for k in range(NC):
+        for cp in aa[k * (R - 1):(k + 1) * (R - 1)]:
+            cp.wait_recv()
         zrt[c, k] = zr_own[:, k * chunk:(k + 1) * chunk].T
 
         @pl.when(hi)
@@ -143,9 +146,19 @@
         def _():
             down(0, k).start()
 
-    ga = []
-    for d in range(1, R):
-        ga.append(rowcopy(zcol.at[r], zcol.at[r], s_ga.at[d], r_ga.at[d], d))
+    relay = R == 4
+
+    def gather(k, d):
+        piece = zcol.at[r, :, pl.ds(pl.multiple_of(k * chunk, 128), chunk)]
+        return rowcopy(piece, piece, s_ga.at[k, d], r_ga.at[k, d], d)
+
+    def forward(k, via, to):
+        piece = zcol.at[flip(r, via), :, pl.ds(pl.multiple_of(k * chunk, 128), chunk)]
+        return rowcopy(piece, piece, s_ga.at[k, R - 1], r_ga.at[k, R - 1], to)
+
+    direct = R - 1 if relay else R
+    for d in range(1, direct):
+        gather(0, d).start()
 
     tot = zw[0].astype(F32)
     for cp in zc:
@@ -157,23 +170,25 @@
     for d in range(1, R):
         zr.append(rowcopy(zwr.at[0], zwr.at[d], s_zr.at[d], r_zr.at[d], d))
         zr[-1].start()
-    for cp in ga:
-        cp.start()
+    for k in range(1, NC):
+        for d in range(1, direct):
+            gather(k, d).start()
     for cp in zr:
         cp.wait_recv()
     for d in range(R):
         zwt[pl.ds(pl.multiple_of(flip(r, d) * pad, 16), pad), :] = zwr[d]
-    zt[...] = zwt[...].T
 
     def compute(i, k, d_lo, d_hi):
-        pbuf[0:W, :] = power_eight(dot(zt[...], zrt[i, k], ((1,), (1,)))).astype(BF16)
-
         def one(d, _):
             j = flip(r, d)
             adj = power_eight(dot(zrt[i, k], zcol[j])).astype(BF16)
-            macc[j] += dot(pbuf[...], adj)
+            macc[j] += dot(pbuf[i, k], adj)
             return 0
         lax.fori_loop(d_lo, d_hi, one, 0)
+
+    def panel(i, k):
+        pt = power_eight(dot(zrt[i, k], zwt[...])).T
+        pbuf[i, k, 0:W, :] = pt.astype(BF16)
 
     def arrive(s, k):
         @pl.when(c - s >= 0)
@@ -201,6 +216,9 @@
 
                 @pl.when((i >= 0) & (i < C))
                 def _():
+                    @pl.when(start(t) == 0)
+                    def _():
+                        panel(i, k)
                     compute(i, k, start(t), d_hi)
                 return 0
             lax.fori_loop(t_lo, t_hi, each, 0)
@@ -208,18 +226,21 @@
         lax.fori_loop(0, NC, step, 0)
 
     def own(k, _):
+        panel(c, k)
         compute(c, k, 0, 1)
         return 0
     lax.fori_loop(0, NC, own, 0)
 
-    def pass_on(k, _):
+    for k in range(NC):
         arrive(1, k)
-        return 0
-    lax.fori_loop(0, NC, pass_on, 0)
-    for cp in ga[:-1]:
-        cp.wait_recv()
+        for d in range(1, R - 1):
+            gather(k, d).wait_recv()
+        if relay:
+            via = 1 if k < NC // 2 else 2
+            forward(k, via, 3 - via).start()
     phase(2, 0, 3, lambda t: jnp.where(t == 0, 1, 0), R - 1)
-    ga[-1].wait_recv()
+    for k in range(NC):
+        gather(k, R - 1).wait_recv()
     phase(3, 0, 7, lambda t: jnp.where(t < 3, R - 1, 0), R)
     if C > 4:
         def later(s, _):
@@ -258,8 +279,11 @@
             total = total + degr[d, j]
         dego[:, j * slab:(j + 1) * slab] = total
 
-    for cp in st + aa + zc + zr + ga + out_cp + dg:
+    for cp in st + aa + zc + zr + out_cp + dg:
         cp.wait_send()
+    for k in range(NC):
+        for d in range(1, R):
+            gather(k, d).wait_send()
 
     def drain(s, _):
         def each(k, _):
@@ -303,13 +327,12 @@
                 V((C, pad, W), BF16),
                 V((R, pad, W), BF16),
                 V((R * pad, W), BF16),
-                V((W, R * pad), BF16),
-                V((W + 16, chunk), BF16),
+                V((C, NC, W + 16, chunk), BF16),
                 V((R, W + 16, slab), F32),
                 V((R, R, W // R, slab), F32),
                 V((R, 1, slab), F32),
                 V((R, R, 1, slab), F32),
-                dma((R,)), dma((R,)), dma((R,)), dma((R,)), dma((R,)), dma((R,)),
+                dma((R,)), dma((R,)), dma((NC, R)), dma((NC, R)), dma((NC, R)), dma((NC, R)),
                 dma((C,)), dma((C,)), dma((R,)), dma((R,)),
                 dma((C, NC)), dma((C, NC)), dma((C, NC)), dma((C, NC)),
                 dma((R, R)), dma((R, R)), dma((R,)), dma((R,)),

time: 188 us -> 171 us (0.910)
  Pallas kernels: 183 us -> 166 us
    pallas_call x1, Pallas kernels: 183 us -> 166 us  [body(): pl.pallas_call(functools.partial(kernel, R, C, 1e-06), out_shape=(jax.Sha...]
where the time goes in v2:
time: 171 us
  Pallas kernels  166 us (97%)
  local copies, waits for them, and re-layouts  3.59 us (2%)
    pallas_call x1, Pallas kernels, body(): pl.pallas_call(functools.partial(kernel, R, C, 1e-06), out_shape=(jax.Sha...  166 us
    unnamed x2, local copies, waits for them, and re-layouts  3.59 us

profile of v2, /device:TPU:2, one launch (start us, length us, event | category | flops | bytes accessed | tf_op | source)
XLA Modules:
  0.0 170.6 jit_solution(12129117435905630273)
XLA Ops:
  0.6 166.4 %shard_map.41 = (f32[64,4096]{1,0:T(8,128)}, f32[1,4096]{1,0:T(1,128)}) custom-call(f32[150,4096]{1,0:T(8,128)} %expr.1, s32[1,256]{1,0:T(1,128)} %bitcast.3), custom_call_target="tpu_custom_call" | custom-call | tf_op jit(solution)/shard_map/pallas_call | solution.py:316
  167.0 2.3 %copy.6 = f32[64,4096]{1,0:T(8,128)} copy(f32[64,4096]{1,0:T(8,128)} %get-tuple-element.8) | data formatting | bytes 2097152
  169.3 1.3 copy.7
